TPU v7x, 64 devices: a 2x2x8 block of a 4x4x8 slice. The times are simulated.
64 devices in a mesh: data: 4 (over x, y), tp: 16 (over z, core).
Axes of the slice: x: 2, y: 2, z: 8, core: 2. Of those that a mesh axis runs over, the one named last changes fastest.
The devices are a block of a 4x4x8 slice.
Arguments:
- x: bfloat16 [1024, 49152], P('data', 'tp'), parts along dimension 0
- w: bfloat16 [49152, 12288], P('tp')
- lengths: int32 [16], P('data'), parts along dimension 0
Outputs:
- output: bfloat16 [1024, 12288], P('data'), parts along dimension 0
There are 4 independent parts. A program takes and returns all parts, laid end to end along the dimension named above; an argument that names none is the same for every part.
All inputs are finite; a program needn't handle non-finite values.
Results may differ from a plain program's by a relative error of at most 0.001.
Values are sent between devices in bfloat16 or wider.
A program may use at most 768 MiB of HBM per device.

v0:
```python
import jax
import jax.numpy as jnp
from jax import lax
from jax.sharding import PartitionSpec as P


def solution(mesh):
    tp_size = mesh.shape["tp"]

    def local_part(x_loc, w_loc, lengths):
        tokens = x_loc.shape[0]
        seq_len = tokens // lengths.shape[0]
        rows_dev = tokens // tp_size
        part_sum = jnp.dot(x_loc, w_loc, preferred_element_type=jnp.float32)
        own_rows = lax.psum_scatter(part_sum, "tp", scatter_dimension=0, tiled=True)
        valid = (jnp.arange(seq_len, dtype=jnp.int32)[None, :] < lengths[:, None]).reshape(-1)
        own_valid = lax.dynamic_slice_in_dim(valid, lax.axis_index("tp") * rows_dev, rows_dev)
        own_out = jnp.where(own_valid[:, None], own_rows, 0.0).astype(jnp.bfloat16)
        return lax.all_gather(own_out, "tp", axis=0, tiled=True)

    return jax.shard_map(local_part, mesh=mesh, in_specs=(P("data", "tp"), P("tp", None), P("data")), out_specs=P("data", None), check_vma=False)
```

profile of v0, /device:TPU:21, one launch (start us, length us, event | category | flops | bytes accessed | tf_op | source)
XLA Modules:
  0.0 180.3 jit_solution(1305276110497378864)
XLA Ops:
  6.5 0.0 copy-start
  6.6 0.0 reduce-scatter.2.cloned.1.call-start
  6.6 1.4 copy-done
  8.0 33.2 %fusion = f32[256,12288]{1,0:T(8,128)} fusion(bf16[256,3072]{1,0:T(8,128)(2,1)S(1)} %copy-done, bf16[3072,12288]{1,0:T(8,128)(2,1)} %param.4), kind=kOutput, calls=%fused_computation.2 | convolution fusion | flops 19327352832 | bytes 89653248 | tf_op jit(solution)/shard_map/dot_general | solution.py:14
  41.2 0.0 copy-start.1
  41.2 0.1 reduce-scatter.2.cloned.1.call-update
  41.3 0.1 all-gather.2.cloned.1.call-start
  41.3 0.5 copy-done.1
  41.9 0.1 iota_compare_fusion
  41.9 0.1 lt.23
  42.0 0.1 dynamic_slice.3
  42.1 79.4 %reduce-scatter.2.cloned.1.call-done = f32[16,12288]{1,0:T(8,128)} async-done(((f32[256,12288]{1,0:T(8,128)}), f32[16,12288]{1,0:T(8,128)}) %reduce-scatter.2.cloned.1.call-update) | async-done | bytes 786448 | tf_op jit(solution)/shard_map/reduce_scatter | solution.py:15
  121.5 2.0 %select_convert_fusion = bf16[16,12288]{1,0:T(8,128)(2,1)} fusion(f32[16,12288]{1,0:T(8,128)} %reduce-scatter.2.cloned.1.call-done, pred[16]{0:T(512)(128)(4,1)S(1)} %dynamic_slice.3), kind=kLoop, calls=%fused_computation | loop fusion | flops 196608 | bytes 1179664 | tf_op jit(solution)/shard_map/convert_element_type | solution.py:18
  123.5 0.1 all-gather.2.cloned.1.call-update
  123.6 43.7 %all-gather.2.cloned.1.call-done = bf16[256,12288]{1,0:T(8,128)(2,1)} async-done(((bf16[16,12288]{1,0:T(8,128)(2,1)}), bf16[256,12288]{1,0:T(8,128)(2,1)}) %all-gather.2.cloned.1.call-update) | async-done | bytes 6291472 | tf_op jit(solution)/shard_map/all_gather | solution.py:19
  167.3 6.1 %copy.5 = bf16[256,12288]{1,0:T(8,128)(2,1)} copy(bf16[256,12288]{1,0:T(8,128)(2,1)} %all-gather.2.cloned.1.call-done) | data formatting | bytes 12582912
Async XLA Ops:
  6.5 1.4 copy-start
  6.6 115.0 %reduce-scatter.2.cloned.1.call-start = ((), (), s32[]{:S(2)}) async-start(), calls=%async_computation.1 | async-start | bytes 13369344 | tf_op jit(solution)/shard_map/reduce_scatter | solution.py:15
  41.2 0.7 copy-start.1
  41.3 126.0 %all-gather.2.cloned.1.call-start = ((), (), s32[]{:S(2)}) async-start(), calls=%async_computation.2 | async-start | bytes 6684672 | tf_op jit(solution)/shard_map/all_gather | solution.py:19
Sparse Core Ops, SparseCore 0:
  41.4 80.0 reduce-scatter.1
  123.7 43.5 all-gather.1
where the time goes:
time: 181 us; the launch traced here: 180 us
  waiting for transfers between devices  123 us (68%)
  matrix products  33.2 us (18%)
  between operations  13.4 us (7%)
  local copies, waits for them, and re-layouts  8.23 us (5%)
  other arithmetic  2.06 us (1%)
    reduce_scatter x1, waiting for transfers between devices, local_part(): own_rows = lax.psum_scatter(part_sum, 'tp', scatter_dimension=0, tiled=True)  79.4 us
    all_gather x1, waiting for transfers between devices, local_part(): return lax.all_gather(own_out, 'tp', axis=0, tiled=True)  43.7 us
    dot_general x1, matrix products, local_part(): part_sum = jnp.dot(x_loc, w_loc, preferred_element_type=jnp.float32)  33.2 us
    unnamed x5, local copies, waits for them, and re-layouts  8.07 us
  transfers between devices with their start and end apart: 2, of which 2 were waited for; matrix products, arithmetic and copies ran while one was open for 0% of the time, Pallas kernels for 0%

commit v1 on v0

v1 whole, which is shorter than its diff:
```python
import functools

import jax
import jax.numpy as jnp
from jax import lax
from jax.experimental import pallas as pl
from jax.experimental.pallas import tpu as pltpu
from jax.sharding import PartitionSpec as P

MESH = pl.DeviceIdType.MESH
LANES = 128
CORES = 2
DIRS = 2
UNITS = 3
LAG = 3


def first_single(len_ref, n_seq):
    slot = jnp.int32(n_seq - 1)
    for s in reversed(range(n_seq - 1)):
        slot = jnp.where(len_ref[s] == 1, jnp.int32(s), slot)
    return slot


def reduce_kernel(
    chips, n_seq, seq_len,
    len_ref, x_hbm, w_hbm, y_hbm,
    x_raw, xc, wbuf, part, part_in, rs_in, ag, ag_pair,
    x_sem, w_sem, pp_send, pp_recv, rs_send, rs_recv, ag_send, ag_recv, ap_send, ap_recv, out_sem, outp_sem,
):
    me = lax.axis_index("tp")
    z, core = me // CORES, lax.rem(me, CORES)
    nxt = lax.rem(z + 1, chips) * CORES + core
    prv = lax.rem(z + chips - 1, chips) * CORES + core
    mate = z * CORES + (1 - core)
    towards = (nxt, prv)
    body_rows = (n_seq - 1) * seq_len
    lastc = chips - 1
    n_k = DIRS * UNITS

    def chunk_of(s, d):
        if d == 0:
            return lax.rem(z + (2 * chips - 1) - s, chips)
        return lax.rem(z + 1 + s, chips)

    def slot_chunk(h, d):
        if d == 0:
            return lax.rem(z + chips - h, chips)
        return lax.rem(z + h, chips)

    def w_copy(s, k):
        d, u = k % DIRS, k // DIRS
        col = ((chunk_of(s, d) * DIRS + d) * UNITS + u) * (CORES * LANES)
        col = pl.multiple_of(col, CORES * LANES)
        return pltpu.make_async_copy(w_hbm.at[:, pl.ds(col, CORES * LANES)], wbuf.at[k], w_sem.at[k])

    def f_rows(u):
        return pl.ds(u * body_rows, body_rows + (8 if u == UNITS - 1 else 0))

    def h_rows(u):
        return pl.ds(u * body_rows, body_rows + (16 if u == UNITS - 1 else 0))

    x_copy = pltpu.make_async_copy(x_hbm, x_raw, x_sem)
    x_copy.start()
    for k in range(n_k):
        w_copy(0, k).start()

    barrier = pltpu.get_barrier_semaphore()
    for peer in (mate, nxt, prv):
        pl.semaphore_signal(barrier, inc=1, device_id={"tp": peer}, device_id_type=MESH)

    single = first_single(len_ref, n_seq)
    x_copy.wait()
    def x_rows(slot, count):
        return x_raw[slot * seq_len:slot * seq_len + count, :]

    for p in range(n_seq - 1):
        xc[p * seq_len:(p + 1) * seq_len, :] = jnp.where(single <= p, x_rows(p + 1, seq_len), x_rows(p, seq_len))
    lone = x_rows(n_seq - 1, 16)
    for s in range(n_seq - 1):
        lone = jnp.where(single == s, x_rows(s, 16), lone)
    xc[body_rows:body_rows + 16, :] = lone
    pl.semaphore_wait(barrier, 3)

    def pp_copy(s, k):
        d, u = k % DIRS, k // DIRS
        return pltpu.make_async_remote_copy(
            src_ref=part.at[1 - core, s, d, f_rows(u)], dst_ref=part_in.at[s, d, f_rows(u)],
            send_sem=pp_send.at[s, k], recv_sem=pp_recv.at[s, k], device_id={"tp": mate}, device_id_type=MESH)

    def rs_copy(s, k):
        d, u = k % DIRS, k // DIRS
        return pltpu.make_async_remote_copy(
            src_ref=part.at[core, s, d, f_rows(u)], dst_ref=rs_in.at[s, d, f_rows(u)],
            send_sem=rs_send.at[s, k], recv_sem=rs_recv.at[s, k], device_id={"tp": towards[d]}, device_id_type=MESH)

    def ag_copy(h, k):
        d, u = k % DIRS, k // DIRS
        return pltpu.make_async_remote_copy(
            src_ref=ag.at[h, d, h_rows(u)], dst_ref=ag.at[h + 1, d, h_rows(u)],
            send_sem=ag_send.at[h, k], recv_sem=ag_recv.at[h, k], device_id={"tp": towards[d]}, device_id_type=MESH)

    def ap_copy(h, k):
        d, u = k % DIRS, k // DIRS
        return pltpu.make_async_remote_copy(
            src_ref=ag.at[h, d, h_rows(u)], dst_ref=ag_pair.at[h, d, h_rows(u)],
            send_sem=ap_send.at[h, k], recv_sem=ap_recv.at[h, k], device_id={"tp": mate}, device_id_type=MESH)

    def out_copy(h, k):
        d, u = k % DIRS, k // DIRS
        return pltpu.make_async_copy(
            ag.at[h, d, h_rows(u)], y_hbm.at[core, slot_chunk(h, d), d, h_rows(u)], out_sem.at[h, k])

    def outp_copy(h, k):
        d, u = k % DIRS, k // DIRS
        return pltpu.make_async_copy(
            ag_pair.at[h, d, h_rows(u)], y_hbm.at[1 - core, slot_chunk(h, d), d, h_rows(u)], outp_sem.at[h, k])

    def compute(s, k):
        d, u = k % DIRS, k // DIRS
        w_copy(s, k).wait()
        prod = jnp.dot(xc[...], wbuf[k], preferred_element_type=jnp.float32)
        for half in range(CORES):
            cols = slice(half * LANES, (half + 1) * LANES)
            part[half, s, d, u * body_rows:(u + 1) * body_rows, :] = prod[:body_rows, cols]
            tile = UNITS * body_rows
            if u == 0:
                part[half, s, d, tile:tile + 8, :] = prod[body_rows:body_rows + 8, cols]
            else:
                part[half, s, d, tile + u:tile + u + 1, :] = prod[body_rows:body_rows + 1, cols]
        pp_copy(s, k).start()

        @pl.when(s < lastc)
        def _():
            w_copy(s + 1, k).start()

    def ring(s, k):
        d, u = k % DIRS, k // DIRS
        rows = f_rows(u)
        pp_copy(s, k).wait_recv()

        @pl.when(s == 0)
        def _():
            part[core, s, d, rows, :] = part[core, s, d, rows, :] + part_in[s, d, rows, :]
            rs_copy(s, k).start()

        @pl.when(jnp.logical_and(s > 0, s < lastc))
        def _():
            rs_copy(s - 1, k).wait_recv()
            part[core, s, d, rows, :] = (part[core, s, d, rows, :] + part_in[s, d, rows, :]) + rs_in[s - 1, d, rows, :]
            rs_copy(s, k).start()

        @pl.when(s == lastc)
        def _():
            rs_copy(s - 1, k).wait_recv()
            total = (part[core, s, d, rows, :] + part_in[s, d, rows, :]) + rs_in[s - 1, d, rows, :]
            if u == UNITS - 1:
                total = jnp.concatenate([total, total[body_rows:, :]], axis=0)
            ag[0, d, h_rows(u), :] = total.astype(jnp.bfloat16)
            ag_copy(0, k).start()
            ap_copy(0, k).start()
            out_copy(0, k).start()

    @pl.loop(0, chips)
    def _(s):
        for k in range(n_k):
            compute(s, k)
            if k >= LAG:
                ring(s, k - LAG)
            else:
                @pl.when(s > 0)
                def _():
                    ring(s - 1, k + n_k - LAG)

    for k in range(n_k - LAG, n_k):
        ring(jnp.int32(lastc), k)

    @pl.loop(1, chips)
    def _(h):
        for k in range(n_k):
            ag_copy(h - 1, k).wait_recv()

            @pl.when(h < lastc)
            def _():
                ag_copy(h, k).start()

            ap_copy(h, k).start()
            out_copy(h, k).start()
            ap_copy(h - 1, k).wait_recv()
            outp_copy(h - 1, k).start()

    for k in range(n_k):
        ap_copy(lastc, k).wait_recv()
        outp_copy(lastc, k).start()

    @pl.loop(0, chips)
    def _(s):
        for k in range(n_k):
            pp_copy(s, k).wait_send()
            ap_copy(s, k).wait_send()
            out_copy(s, k).wait()
            outp_copy(s, k).wait()

            @pl.when(s < lastc)
            def _():
                rs_copy(s, k).wait_send()
                ag_copy(s, k).wait_send()


def expand_kernel(n_seq, seq_len, len_ref, y_ref, o_ref):
    body_rows = (n_seq - 1) * seq_len
    single = first_single(len_ref, n_seq)
    row = lax.broadcasted_iota(jnp.int32, (seq_len, LANES), 0)
    for u in range(UNITS):
        for core in range(CORES):
            cols = slice((u * CORES + core) * LANES, (u * CORES + core + 1) * LANES)
            tile = y_ref[core, 0, 0, UNITS * body_rows:UNITS * body_rows + 16, :].astype(jnp.float32)
            lone = jnp.broadcast_to(tile[u:u + 1, :], (seq_len, LANES))
            for s in range(n_seq):
                pos = jnp.minimum(s - (single < s).astype(jnp.int32), n_seq - 2)
                start = pl.multiple_of(u * body_rows + pos * seq_len, seq_len)
                rows = y_ref[core, 0, 0, pl.ds(start, seq_len), :].astype(jnp.float32)
                rows = jnp.where(single == s, lone, rows)
                o_ref[s * seq_len:(s + 1) * seq_len, cols] = jnp.where(row < len_ref[s], rows, 0.0).astype(o_ref.dtype)


def solution(mesh):
    chips = mesh.shape["tp"] // CORES

    def local_part(x_loc, w_loc, lengths):
        tokens, depth = x_loc.shape
        columns = w_loc.shape[1]
        n_seq = lengths.shape[0]
        seq_len = tokens // n_seq
        body_rows = (n_seq - 1) * seq_len
        n_k = DIRS * UNITS
        assert columns == chips * DIRS * UNITS * CORES * LANES
        f_tall, h_tall = UNITS * body_rows + 8, UNITS * body_rows + 16
        dma = pltpu.SemaphoreType.DMA
        packed = pl.pallas_call(
            functools.partial(reduce_kernel, chips, n_seq, seq_len),
            out_shape=jax.ShapeDtypeStruct((CORES, chips, DIRS, h_tall, LANES), jnp.bfloat16),
            in_specs=[
                pl.BlockSpec(memory_space=pltpu.SMEM),
                pl.BlockSpec(memory_space=pl.ANY),
                pl.BlockSpec(memory_space=pl.ANY),
            ],
            out_specs=pl.BlockSpec(memory_space=pl.ANY),
            scratch_shapes=[
                pltpu.VMEM((tokens, depth), jnp.bfloat16),
                pltpu.VMEM((body_rows + 16, depth), jnp.bfloat16),
                pltpu.VMEM((n_k, depth, CORES * LANES), jnp.bfloat16),
                pltpu.VMEM((CORES, chips, DIRS, f_tall, LANES), jnp.float32),
                pltpu.VMEM((chips, DIRS, f_tall, LANES), jnp.float32),
                pltpu.VMEM((chips - 1, DIRS, f_tall, LANES), jnp.float32),
                pltpu.VMEM((chips, DIRS, h_tall, LANES), jnp.bfloat16),
                pltpu.VMEM((chips, DIRS, h_tall, LANES), jnp.bfloat16),
                dma,
                dma((n_k,)),
                dma((chips, n_k)), dma((chips, n_k)),
                dma((chips - 1, n_k)), dma((chips - 1, n_k)),
                dma((chips - 1, n_k)), dma((chips - 1, n_k)),
                dma((chips, n_k)), dma((chips, n_k)),
                dma((chips, n_k)), dma((chips, n_k)),
            ],
            compiler_params=pltpu.CompilerParams(
                collective_id=0, has_side_effects=True, vmem_limit_bytes=60 * 1024 * 1024),
            name="reduce_gather",
        )(lengths, x_loc, w_loc)
        wide = UNITS * CORES * LANES
        return pl.pallas_call(
            functools.partial(expand_kernel, n_seq, seq_len),
            out_shape=jax.ShapeDtypeStruct((tokens, columns), jnp.bfloat16),
            grid=(chips * DIRS,),
            in_specs=[
                pl.BlockSpec(memory_space=pltpu.SMEM),
                pl.BlockSpec((CORES, 1, 1, h_tall, LANES), lambda i: (0, i // DIRS, i % DIRS, 0, 0)),
            ],
            out_specs=pl.BlockSpec((tokens, wide), lambda i: (0, i)),
            name="expand_rows",
        )(lengths, packed)

    return jax.shard_map(local_part, mesh=mesh, in_specs=(P("data", "tp"), P("tp", None), P("data")), out_specs=P("data", None), check_vma=False)
```

time: 181 us -> 105 us (0.58)
  waiting for transfers between devices: 123 us -> 0 us
  Pallas kernels: 0 us -> 105 us
  matrix products: 33.2 us -> 0 us
  between operations: 13.4 us -> 0.01 us
  local copies, waits for them, and re-layouts: 8.23 us -> 0 us
  other arithmetic: 2.06 us -> 0 us
    pallas_call x0 -> x2, Pallas kernels: none -> 105 us  [the longest x1 93.1 us: local_part(): pl.pallas_call(functools.partial(reduce_kernel, chips, n_seq, seq_len), o...]
    reduce_scatter x1 -> x0, waiting for transfers between devices: 79.4 us -> none  [local_part(): own_rows = lax.psum_scatter(part_sum, 'tp', scatter_dimension=0, tiled=True)]
    all_gather x1 -> x0, waiting for transfers between devices: 43.7 us -> none  [local_part(): return lax.all_gather(own_out, 'tp', axis=0, tiled=True)]
    dot_general x1 -> x0, matrix products: 33.2 us -> none  [local_part(): part_sum = jnp.dot(x_loc, w_loc, preferred_element_type=jnp.float32)]
    unnamed x5 -> x0, local copies, waits for them, and re-layouts: 8.07 us -> none
    convert_element_type x1 -> x0, other arithmetic: 1.99 us -> none  [local_part(): own_out = jnp.where(own_valid[:, None], own_rows, 0.0).astype(jnp.bfloat16)]
  transfers between devices with their start and end apart: 2 -> 0, of which waited for: 2 -> 0; matrix products, arithmetic and copies ran while one was open for 0% -> 0% of each run, Pallas kernels for 0% -> 0%
where the time goes in v1:
time: 105 us
  Pallas kernels  105 us (100%)
    pallas_call x1, Pallas kernels, local_part(): pl.pallas_call(functools.partial(reduce_kernel, chips, n_seq, seq_len), o...  93.1 us
    pallas_call x1, Pallas kernels, local_part(): pl.pallas_call(functools.partial(expand_kernel, n_seq, seq_len), out_shap...  11.7 us

profile of v1, /device:TPU:21, one launch (start us, length us, event | category | flops | bytes accessed | tf_op | source)
XLA Modules:
  0.0 104.8 jit_solution(4827439435121678236)
XLA Ops:
  0.0 93.1 %reduce_gather.1.y_ref = bf16[2,8,2,592,128]{4,3,2,1,0:T(8,128)(2,1)} custom-call(s32[4]{0:T(128)} %len_ref.3, bf16[256,3072]{1,0:T(8,128)(2,1)} %x_hbm.1, bf16[3072,12288]{1,0:T(8,128)(2,1)} %w_hbm.1), custom_call_target="tpu_custom_call" | custom-call | tf_op jit(solution)/shard_map/reduce_gather/pallas_call | solution.py:240
  93.1 11.7 %expand_rows.1 = bf16[256,12288]{1,0:T(8,128)(2,1)} custom-call(s32[4]{0:T(128)} %len_ref.3, bf16[2,8,2,592,128]{4,3,2,1,0:T(8,128)(2,1)} %reduce_gather.1.y_ref), custom_call_target="tpu_custom_call" | custom-call | tf_op jit(solution)/shard_map/expand_rows/pallas_call | solution.py:271

commit v2 on v1

v2 whole, which is shorter than its diff:
```python
import functools

import jax
import jax.numpy as jnp
from jax import lax
from jax.experimental import pallas as pl
from jax.experimental.pallas import tpu as pltpu
from jax.sharding import PartitionSpec as P

MESH = pl.DeviceIdType.MESH
LANES = 128
CORES = 2
DIRS = 2
UNITS = 3


def first_single(len_ref, n_seq):
    slot = jnp.int32(n_seq - 1)
    for s in reversed(range(n_seq - 1)):
        slot = jnp.where(len_ref[s] == 1, jnp.int32(s), slot)
    return slot


def reduce_kernel(
    chips, n_seq, seq_len,
    len_ref, x_hbm, w_hbm, ag, ag_pair,
    x_raw, xc, wbuf, part, part_in, rs_in,
    x_sem, w_sem, pp_send, pp_recv, rs_send, rs_recv, ag_send, ag_recv, ap_send, ap_recv,
):
    me = lax.axis_index("tp")
    z, core = me // CORES, lax.rem(me, CORES)
    nxt = lax.rem(z + 1, chips) * CORES + core
    prv = lax.rem(z + chips - 1, chips) * CORES + core
    mate = z * CORES + (1 - core)
    towards = (nxt, prv)
    body_rows = (n_seq - 1) * seq_len
    lastc = chips - 1
    n_k = DIRS * UNITS

    def chunk_of(s, d):
        if d == 0:
            return lax.rem(z + (2 * chips - 1) - s, chips)
        return lax.rem(z + 1 + s, chips)

    def w_copy(s, k):
        d, u = k % DIRS, k // DIRS
        col = ((chunk_of(s, d) * DIRS + d) * UNITS + u) * (CORES * LANES)
        col = pl.multiple_of(col, CORES * LANES)
        return pltpu.make_async_copy(w_hbm.at[:, pl.ds(col, CORES * LANES)], wbuf.at[u, :, pl.ds(d * CORES * LANES, CORES * LANES)], w_sem.at[k])

    def f_rows(u):
        return pl.ds(u * body_rows, body_rows + (8 if u == UNITS - 1 else 0))

    def h_rows(u):
        return pl.ds(u * body_rows, body_rows + (16 if u == UNITS - 1 else 0))

    x_copy = pltpu.make_async_copy(x_hbm, x_raw, x_sem)
    x_copy.start()
    for k in range(n_k):
        w_copy(0, k).start()

    barrier = pltpu.get_barrier_semaphore()
    for peer in (mate, nxt, prv):
        pl.semaphore_signal(barrier, inc=1, device_id={"tp": peer}, device_id_type=MESH)

    single = first_single(len_ref, n_seq)
    x_copy.wait()
    def x_rows(slot, count):
        return x_raw[slot * seq_len:slot * seq_len + count, :]

    for p in range(n_seq - 1):
        xc[p * seq_len:(p + 1) * seq_len, :] = jnp.where(single <= p, x_rows(p + 1, seq_len), x_rows(p, seq_len))
    lone = x_rows(n_seq - 1, 16)
    for s in range(n_seq - 1):
        lone = jnp.where(single == s, x_rows(s, 16), lone)
    xc[body_rows:body_rows + 16, :] = lone
    pl.semaphore_wait(barrier, 3)

    def pp_copy(s, k):
        d, u = k % DIRS, k // DIRS
        return pltpu.make_async_remote_copy(
            src_ref=part.at[1 - core, s, d, f_rows(u)], dst_ref=part_in.at[s, d, f_rows(u)],
            send_sem=pp_send.at[s, k], recv_sem=pp_recv.at[s, k], device_id={"tp": mate}, device_id_type=MESH)

    def rs_copy(s, k):
        d, u = k % DIRS, k // DIRS
        return pltpu.make_async_remote_copy(
            src_ref=part.at[core, s, d, f_rows(u)], dst_ref=rs_in.at[s, d, f_rows(u)],
            send_sem=rs_send.at[s, k], recv_sem=rs_recv.at[s, k], device_id={"tp": towards[d]}, device_id_type=MESH)

    def ag_copy(h, k):
        d, u = k % DIRS, k // DIRS
        return pltpu.make_async_remote_copy(
            src_ref=ag.at[h, d, h_rows(u)], dst_ref=ag.at[h + 1, d, h_rows(u)],
            send_sem=ag_send.at[h, k], recv_sem=ag_recv.at[h, k], device_id={"tp": towards[d]}, device_id_type=MESH)

    def ap_copy(h, k):
        d, u = k % DIRS, k // DIRS
        return pltpu.make_async_remote_copy(
            src_ref=ag.at[h, d, h_rows(u)], dst_ref=ag_pair.at[h, d, h_rows(u)],
            send_sem=ap_send.at[h, k], recv_sem=ap_recv.at[h, k], device_id={"tp": mate}, device_id_type=MESH)

    def compute(s, u):
        for d in range(DIRS):
            w_copy(s, u * DIRS + d).wait()
        prod = jnp.dot(xc[...], wbuf[u], preferred_element_type=jnp.float32)
        for d in range(DIRS):
            for half in range(CORES):
                cols = slice((d * CORES + half) * LANES, (d * CORES + half + 1) * LANES)
                part[half, s, d, u * body_rows:(u + 1) * body_rows, :] = prod[:body_rows, cols]
                tile = UNITS * body_rows
                if u == 0:
                    part[half, s, d, tile:tile + 8, :] = prod[body_rows:body_rows + 8, cols]
                else:
                    part[half, s, d, tile + u:tile + u + 1, :] = prod[body_rows:body_rows + 1, cols]
            pp_copy(s, u * DIRS + d).start()

        @pl.when(s < lastc)
        def _():
            for d in range(DIRS):
                w_copy(s + 1, u * DIRS + d).start()

    def ring(s, k):
        d, u = k % DIRS, k // DIRS
        rows = f_rows(u)
        pp_copy(s, k).wait_recv()

        @pl.when(s == 0)
        def _():
            part[core, s, d, rows, :] = part[core, s, d, rows, :] + part_in[s, d, rows, :]
            rs_copy(s, k).start()

        @pl.when(jnp.logical_and(s > 0, s < lastc))
        def _():
            rs_copy(s - 1, k).wait_recv()
            part[core, s, d, rows, :] = (part[core, s, d, rows, :] + part_in[s, d, rows, :]) + rs_in[s - 1, d, rows, :]
            rs_copy(s, k).start()

        @pl.when(s == lastc)
        def _():
            rs_copy(s - 1, k).wait_recv()
            total = (part[core, s, d, rows, :] + part_in[s, d, rows, :]) + rs_in[s - 1, d, rows, :]
            if u == UNITS - 1:
                total = jnp.concatenate([total, total[body_rows:, :]], axis=0)
            ag[0, d, h_rows(u), :] = total.astype(jnp.bfloat16)
            ag_copy(0, k).start()
            ap_copy(0, k).start()

    def ring_pair(s, u):
        for d in range(DIRS):
            ring(s, u * DIRS + d)

    @pl.loop(0, chips)
    def _(s):
        for u in range(UNITS):
            compute(s, u)
            if u > 0:
                ring_pair(s, u - 1)
            else:
                @pl.when(s > 0)
                def _():
                    ring_pair(s - 1, UNITS - 1)

    ring_pair(jnp.int32(lastc), UNITS - 1)

    @pl.loop(1, chips)
    def _(h):
        for k in range(n_k):
            ag_copy(h - 1, k).wait_recv()

            @pl.when(h < lastc)
            def _():
                ag_copy(h, k).start()

            ap_copy(h, k).start()

    @pl.loop(0, chips)
    def _(s):
        for k in range(n_k):
            pp_copy(s, k).wait_send()
            ap_copy(s, k).wait()

            @pl.when(s < lastc)
            def _():
                rs_copy(s, k).wait_send()
                ag_copy(s, k).wait_send()


def expand_kernel(chips, n_seq, seq_len, len_ref, ag, ag_pair, o_hbm, keep, alone, stage, sems):
    me = lax.axis_index("tp")
    z, core = me // CORES, lax.rem(me, CORES)
    body_rows = (n_seq - 1) * seq_len
    single = first_single(len_ref, n_seq)
    row = lax.broadcasted_iota(jnp.int32, (seq_len, LANES), 0)
    for s in range(n_seq):
        many = jnp.where(single == s, 0, len_ref[s])
        one = jnp.where(single == s, 1, 0)
        keep[s * seq_len:(s + 1) * seq_len, :] = jnp.where(row < many, 1.0, 0.0).astype(jnp.bfloat16)
        alone[s * 16:(s + 1) * 16, :] = jnp.where(row[:16] < one, 1.0, 0.0).astype(jnp.bfloat16)
    zero = jnp.bfloat16(0)

    def out_copy(h, d):
        chunk = lax.rem(z + chips - h, chips) if d == 0 else lax.rem(z + h, chips)
        wide = UNITS * CORES * LANES
        cols = pl.ds(pl.multiple_of((chunk * DIRS + d) * wide, wide), wide)
        return pltpu.make_async_copy(stage.at[h, d], o_hbm.at[:, cols], sems.at[h, d])

    @pl.loop(0, chips)
    def _(h):
        for d in range(DIRS):
            for near, ref in enumerate((ag, ag_pair)):
                side = core if near == 0 else 1 - core
                tile = ref[h, d, UNITS * body_rows:UNITS * body_rows + 16, :].astype(jnp.float32)
                for u in range(UNITS):
                    cols = pl.ds(pl.multiple_of((u * CORES + side) * LANES, LANES), LANES)
                    lone = jnp.broadcast_to(tile[u:u + 1, :], (16, LANES)).astype(jnp.bfloat16)
                    for s in range(n_seq):
                        pos = jnp.minimum(s - (single < s).astype(jnp.int32), n_seq - 2)
                        start = pl.multiple_of(u * body_rows + pos * seq_len, seq_len)
                        rows = ref[h, d, pl.ds(start, seq_len), :]
                        mask = keep[s * seq_len:(s + 1) * seq_len, :]
                        first = jnp.where(alone[s * 16:(s + 1) * 16, :] > zero, lone, zero)
                        base = s * seq_len
                        stage[h, d, base:base + 16, cols] = jnp.where(mask[:16] > zero, rows[:16], first)
                        stage[h, d, base + 16:base + seq_len, cols] = jnp.where(mask[16:] > zero, rows[16:], zero)
            out_copy(h, d).start()

    @pl.loop(0, chips)
    def _(h):
        for d in range(DIRS):
            out_copy(h, d).wait()


def solution(mesh):
    chips = mesh.shape["tp"] // CORES

    def local_part(x_loc, w_loc, lengths):
        tokens, depth = x_loc.shape
        columns = w_loc.shape[1]
        n_seq = lengths.shape[0]
        seq_len = tokens // n_seq
        body_rows = (n_seq - 1) * seq_len
        n_k = DIRS * UNITS
        assert columns == chips * DIRS * UNITS * CORES * LANES
        f_tall, h_tall = UNITS * body_rows + 8, UNITS * body_rows + 16
        dma = pltpu.SemaphoreType.DMA
        held = pltpu.VMEM((chips, DIRS, h_tall, LANES), jnp.bfloat16)
        vmem = pl.BlockSpec(memory_space=pltpu.VMEM)
        smem = pl.BlockSpec(memory_space=pltpu.SMEM)
        hbm = pl.BlockSpec(memory_space=pl.ANY)
        near, far = pl.pallas_call(
            functools.partial(reduce_kernel, chips, n_seq, seq_len),
            out_shape=(held, held),
            in_specs=[smem, hbm, hbm],
            out_specs=(vmem, vmem),
            scratch_shapes=[
                pltpu.VMEM((tokens, depth), jnp.bfloat16),
                pltpu.VMEM((body_rows + 16, depth), jnp.bfloat16),
                pltpu.VMEM((UNITS, depth, DIRS * CORES * LANES), jnp.bfloat16),
                pltpu.VMEM((CORES, chips, DIRS, f_tall, LANES), jnp.float32),
                pltpu.VMEM((chips, DIRS, f_tall, LANES), jnp.float32),
                pltpu.VMEM((chips - 1, DIRS, f_tall, LANES), jnp.float32),
                dma,
                dma((n_k,)),
                dma((chips, n_k)), dma((chips, n_k)),
                dma((chips - 1, n_k)), dma((chips - 1, n_k)),
                dma((chips - 1, n_k)), dma((chips - 1, n_k)),
                dma((chips, n_k)), dma((chips, n_k)),
            ],
            compiler_params=pltpu.CompilerParams(
                collective_id=0, has_side_effects=True, vmem_limit_bytes=48 * 1024 * 1024),
            name="reduce_gather",
        )(lengths, x_loc, w_loc)
        return pl.pallas_call(
            functools.partial(expand_kernel, chips, n_seq, seq_len),
            out_shape=jax.ShapeDtypeStruct((tokens, columns), jnp.bfloat16),
            in_specs=[smem, vmem, vmem],
            out_specs=hbm,
            scratch_shapes=[
                pltpu.VMEM((tokens, LANES), jnp.bfloat16),
                pltpu.VMEM((n_seq * 16, LANES), jnp.bfloat16),
                pltpu.VMEM((chips, DIRS, tokens, UNITS * CORES * LANES), jnp.bfloat16),
                dma((chips, DIRS)),
            ],
            compiler_params=pltpu.CompilerParams(vmem_limit_bytes=32 * 1024 * 1024),
            name="expand_rows",
        )(lengths, near, far)

    return jax.shard_map(local_part, mesh=mesh, in_specs=(P("data", "tp"), P("tp", None), P("data")), out_specs=P("data", None), check_vma=False)
```

time: 105 us -> 94.1 us (0.90)
  Pallas kernels: 105 us -> 93.3 us
    pallas_call x1, Pallas kernels: 11.7 us -> 3.64 us  [local_part(): pl.pallas_call(functools.partial(expand_kernel, chips, n_seq, seq_len), o...]
    pallas_call x1, Pallas kernels: 93.1 us -> 89.7 us  [local_part(): pl.pallas_call(functools.partial(reduce_kernel, chips, n_seq, seq_len), o...]
where the time goes in v2:
time: 94.1 us; the launch traced here: 94 us
  Pallas kernels  93.3 us (99%)
    pallas_call x1, Pallas kernels, local_part(): pl.pallas_call(functools.partial(reduce_kernel, chips, n_seq, seq_len), o...  89.7 us
    pallas_call x1, Pallas kernels, local_part(): pl.pallas_call(functools.partial(expand_kernel, chips, n_seq, seq_len), o...  3.64 us

profile of v2, /device:TPU:21, one launch (start us, length us, event | category | flops | bytes accessed | tf_op | source)
XLA Modules:
  0.0 94.0 jit_solution(379425543866807877)
XLA Ops:
  0.0 0.0 copy-start
  0.0 0.7 copy-done
  0.7 89.7 %reduce_gather.1 = (bf16[8,2,592,128]{3,2,1,0:T(8,128)(2,1)S(1)}, bf16[8,2,592,128]{3,2,1,0:T(8,128)(2,1)S(1)}) custom-call(s32[4]{0:T(128)S(1)} %copy-done, bf16[256,3072]{1,0:T(8,128)(2,1)} %x_hbm.1, bf16[3072,12288]{1,0:T(8,128)(2,1)} %w_hbm.1), custom_call_target="tpu_custom_call" | custom-call | tf_op jit(solution)/shard_map/reduce_gather/pallas_call | solution.py:251
  90.4 3.6 %expand_rows.1 = bf16[256,12288]{1,0:T(8,128)(2,1)} custom-call(s32[4]{0:T(128)S(1)} %copy-done, bf16[8,2,592,128]{3,2,1,0:T(8,128)(2,1)S(1)} %get-tuple-element.7.ag, bf16[8,2,592,128]{3,2,1,0:T(8,128)(2,1)S(1)} %get-tuple-element.8.ag_pair), custom_call_target="tpu_custom_call" | custom-call | tf_op jit(solution)/shard_map/expand_rows/pallas_call | solution.py:274
Async XLA Ops:
  0.0 0.7 copy-start

commit v3 on v2

--- a/solution.py
+++ b/solution.py
@@ -12,6 +12,7 @@
 CORES = 2
 DIRS = 2
 UNITS = 3
+STEPS = 127 * 256
 
 
 def first_single(len_ref, n_seq):
@@ -21,11 +22,37 @@
     return slot
 
 
+def split_sum(total, rows):
+    high = total.astype(jnp.bfloat16)
+    wide = high.astype(jnp.float32)
+    left = jnp.round((total - wide) / jnp.where(wide == 0.0, 1.0, wide) * STEPS)
+    low = left[:rows // 2] * 256.0 + left[rows // 2:]
+    return high, low.astype(jnp.int32).astype(jnp.int16)
+
+
+def join_sum(high, low):
+    pair = low.astype(jnp.int32).astype(jnp.float32)
+    first = jnp.round(pair * (1.0 / 256.0))
+    left = jnp.concatenate([first, pair - first * 256.0], axis=0)
+    wide = high.astype(jnp.float32)
+    return wide + wide * (left * (1.0 / STEPS))
+
+
+def split_lone(total):
+    high = total.astype(jnp.bfloat16).astype(jnp.float32)
+    return jnp.concatenate([high, total - high], axis=0).astype(jnp.bfloat16)
+
+
+def join_lone(both):
+    both = both.astype(jnp.float32)
+    return both[:8] + both[8:]
+
+
 def reduce_kernel(
     chips, n_seq, seq_len,
     len_ref, x_hbm, w_hbm, ag, ag_pair,
-    x_raw, xc, wbuf, part, part_in, rs_in,
-    x_sem, w_sem, pp_send, pp_recv, rs_send, rs_recv, ag_send, ag_recv, ap_send, ap_recv,
+    x_raw, xc, wbuf, part, part_in, tx_hi, tx_lo, rx_hi, rx_lo,
+    x_sem, w_sem, pp_send, pp_recv, hi_send, hi_recv, lo_send, lo_recv, ag_send, ag_recv, ap_send, ap_recv,
 ):
     me = lax.axis_index("tp")
     z, core = me // CORES, lax.rem(me, CORES)
@@ -54,6 +81,14 @@
     def h_rows(u):
         return pl.ds(u * body_rows, body_rows + (16 if u == UNITS - 1 else 0))
 
+    def b_rows(u):
+        return pl.ds(u * body_rows, body_rows)
+
+    def l_rows(u):
+        return pl.ds(u * (body_rows // 2), body_rows // 2)
+
+    f_tail, h_tail = pl.ds(UNITS * body_rows, 8), pl.ds(UNITS * body_rows, 16)
+
     x_copy = pltpu.make_async_copy(x_hbm, x_raw, x_sem)
     x_copy.start()
     for k in range(n_k):
@@ -82,11 +117,17 @@
             src_ref=part.at[1 - core, s, d, f_rows(u)], dst_ref=part_in.at[s, d, f_rows(u)],
             send_sem=pp_send.at[s, k], recv_sem=pp_recv.at[s, k], device_id={"tp": mate}, device_id_type=MESH)
 
-    def rs_copy(s, k):
-        d, u = k % DIRS, k // DIRS
-        return pltpu.make_async_remote_copy(
-            src_ref=part.at[core, s, d, f_rows(u)], dst_ref=rs_in.at[s, d, f_rows(u)],
-            send_sem=rs_send.at[s, k], recv_sem=rs_recv.at[s, k], device_id={"tp": towards[d]}, device_id_type=MESH)
+    def hi_copy(s, k):
+        d, u = k % DIRS, k // DIRS
+        return pltpu.make_async_remote_copy(
+            src_ref=tx_hi.at[s, d, h_rows(u)], dst_ref=rx_hi.at[s, d, h_rows(u)],
+            send_sem=hi_send.at[s, k], recv_sem=hi_recv.at[s, k], device_id={"tp": towards[d]}, device_id_type=MESH)
+
+    def lo_copy(s, k):
+        d, u = k % DIRS, k // DIRS
+        return pltpu.make_async_remote_copy(
+            src_ref=tx_lo.at[s, d, l_rows(u)], dst_ref=rx_lo.at[s, d, l_rows(u)],
+            send_sem=lo_send.at[s, k], recv_sem=lo_recv.at[s, k], device_id={"tp": towards[d]}, device_id_type=MESH)
 
     def ag_copy(h, k):
         d, u = k % DIRS, k // DIRS
@@ -122,27 +163,44 @@
 
     def ring(s, k):
         d, u = k % DIRS, k // DIRS
-        rows = f_rows(u)
+        rows, last = b_rows(u), u == UNITS - 1
+
+        def here(where):
+            return part[core, s, d, where, :] + part_in[s, d, where, :]
+
+        def arrived():
+            return join_sum(rx_hi[s - 1, d, rows, :], rx_lo[s - 1, d, l_rows(u), :])
+
+        def arrived_lone():
+            return join_lone(rx_hi[s - 1, d, h_tail, :])
+
+        def send(total, lone):
+            tx_hi[s, d, rows, :], tx_lo[s, d, l_rows(u), :] = split_sum(total, body_rows)
+            if last:
+                tx_hi[s, d, h_tail, :] = split_lone(lone)
+            hi_copy(s, k).start()
+            lo_copy(s, k).start()
+
         pp_copy(s, k).wait_recv()
 
         @pl.when(s == 0)
         def _():
-            part[core, s, d, rows, :] = part[core, s, d, rows, :] + part_in[s, d, rows, :]
-            rs_copy(s, k).start()
+            send(here(rows), here(f_tail) if last else None)
 
         @pl.when(jnp.logical_and(s > 0, s < lastc))
         def _():
-            rs_copy(s - 1, k).wait_recv()
-            part[core, s, d, rows, :] = (part[core, s, d, rows, :] + part_in[s, d, rows, :]) + rs_in[s - 1, d, rows, :]
-            rs_copy(s, k).start()
+            hi_copy(s - 1, k).wait_recv()
+            lo_copy(s - 1, k).wait_recv()
+            send(here(rows) + arrived(), here(f_tail) + arrived_lone() if last else None)
 
         @pl.when(s == lastc)
         def _():
-            rs_copy(s - 1, k).wait_recv()
-            total = (part[core, s, d, rows, :] + part_in[s, d, rows, :]) + rs_in[s - 1, d, rows, :]
-            if u == UNITS - 1:
-                total = jnp.concatenate([total, total[body_rows:, :]], axis=0)
-            ag[0, d, h_rows(u), :] = total.astype(jnp.bfloat16)
+            hi_copy(s - 1, k).wait_recv()
+            lo_copy(s - 1, k).wait_recv()
+            ag[0, d, rows, :] = (here(rows) + arrived()).astype(jnp.bfloat16)
+            if last:
+                lone = here(f_tail) + arrived_lone()
+                ag[0, d, h_tail, :] = jnp.concatenate([lone, lone], axis=0).astype(jnp.bfloat16)
             ag_copy(0, k).start()
             ap_copy(0, k).start()
 
@@ -182,7 +240,8 @@
 
             @pl.when(s < lastc)
             def _():
-                rs_copy(s, k).wait_send()
+                hi_copy(s, k).wait_send()
+                lo_copy(s, k).wait_send()
                 ag_copy(s, k).wait_send()
 
 
@@ -259,10 +318,14 @@
                 pltpu.VMEM((UNITS, depth, DIRS * CORES * LANES), jnp.bfloat16),
                 pltpu.VMEM((CORES, chips, DIRS, f_tall, LANES), jnp.float32),
                 pltpu.VMEM((chips, DIRS, f_tall, LANES), jnp.float32),
-                pltpu.VMEM((chips - 1, DIRS, f_tall, LANES), jnp.float32),
+                pltpu.VMEM((chips - 1, DIRS, h_tall, LANES), jnp.bfloat16),
+                pltpu.VMEM((chips - 1, DIRS, UNITS * body_rows // 2, LANES), jnp.int16),
+                pltpu.VMEM((chips - 1, DIRS, h_tall, LANES), jnp.bfloat16),
+                pltpu.VMEM((chips - 1, DIRS, UNITS * body_rows // 2, LANES), jnp.int16),
                 dma,
                 dma((n_k,)),
                 dma((chips, n_k)), dma((chips, n_k)),
+                dma((chips - 1, n_k)), dma((chips - 1, n_k)),
                 dma((chips - 1, n_k)), dma((chips - 1, n_k)),
                 dma((chips - 1, n_k)), dma((chips - 1, n_k)),
                 dma((chips, n_k)), dma((chips, n_k)),

time: 94.1 us -> 83.8 us (0.89)
  Pallas kernels: 93.3 us -> 83 us
    pallas_call x1, Pallas kernels: 89.7 us -> 79.4 us  [local_part(): pl.pallas_call(functools.partial(reduce_kernel, chips, n_seq, seq_len), o...]
where the time goes in v3:
time: 83.8 us; the launch traced here: 83.7 us
  Pallas kernels  83 us (99%)
    pallas_call x1, Pallas kernels, local_part(): pl.pallas_call(functools.partial(reduce_kernel, chips, n_seq, seq_len), o...  79.4 us
    pallas_call x1, Pallas kernels, local_part(): pl.pallas_call(functools.partial(expand_kernel, chips, n_seq, seq_len), o...  3.64 us

profile of v3, /device:TPU:21, one launch (start us, length us, event | category | flops | bytes accessed | tf_op | source)
XLA Modules:
  0.0 83.7 jit_solution(6528109525875306341)
XLA Ops:
  0.0 0.0 copy-start
  0.0 0.7 copy-done
  0.7 79.4 %reduce_gather.1 = (bf16[8,2,592,128]{3,2,1,0:T(8,128)(2,1)S(1)}, bf16[8,2,592,128]{3,2,1,0:T(8,128)(2,1)S(1)}) custom-call(s32[4]{0:T(128)S(1)} %copy-done, bf16[256,3072]{1,0:T(8,128)(2,1)} %x_hbm.1, bf16[3072,12288]{1,0:T(8,128)(2,1)} %w_hbm.1), custom_call_target="tpu_custom_call" | custom-call | tf_op jit(solution)/shard_map/reduce_gather/pallas_call | solution.py:310
  80.0 3.6 %expand_rows.1 = bf16[256,12288]{1,0:T(8,128)(2,1)} custom-call(s32[4]{0:T(128)S(1)} %copy-done, bf16[8,2,592,128]{3,2,1,0:T(8,128)(2,1)S(1)} %get-tuple-element.7.ag, bf16[8,2,592,128]{3,2,1,0:T(8,128)(2,1)S(1)} %get-tuple-element.8.ag_pair), custom_call_target="tpu_custom_call" | custom-call | tf_op jit(solution)/shard_map/expand_rows/pallas_call | solution.py:337
Async XLA Ops:
  0.0 0.7 copy-start

commit v4 on v0

v4 whole, which is shorter than its diff:
```python
import functools

import jax
import jax.numpy as jnp
from jax import lax
from jax.experimental import pallas as pl
from jax.experimental.pallas import tpu as pltpu
from jax.sharding import PartitionSpec as P

MESH = pl.DeviceIdType.MESH
LANES = 128
CORES = 2
WAYS = 2
UNITS = 3
SLOTS = UNITS * WAYS
BLOCK = CORES * WAYS * LANES
LONE = UNITS * WAYS - 1
STEPS = 127 * 256


def first_single(len_ref, n_seq):
    slot = jnp.int32(n_seq - 1)
    for s in reversed(range(n_seq - 1)):
        slot = jnp.where(len_ref[s] == 1, jnp.int32(s), slot)
    return slot


def split_sum(total, rows):
    high = total.astype(jnp.bfloat16)
    wide = high.astype(jnp.float32)
    left = jnp.round((total - wide) / jnp.where(wide == 0.0, 1.0, wide) * STEPS)
    low = left[:rows // 2] * 256.0 + left[rows // 2:]
    return high, low.astype(jnp.int32).astype(jnp.int16)


def join_sum(high, low):
    pair = low.astype(jnp.int32).astype(jnp.float32)
    first = jnp.round(pair * (1.0 / 256.0))
    left = jnp.concatenate([first, pair - first * 256.0], axis=0)
    wide = high.astype(jnp.float32)
    return wide + wide * (left * (1.0 / STEPS))


def split_lone(total):
    high = total.astype(jnp.bfloat16).astype(jnp.float32)
    return jnp.concatenate([high, total - high], axis=0).astype(jnp.bfloat16)


def join_lone(both):
    both = both.astype(jnp.float32)
    return both[:8] + both[8:]


class Rows:
    def __init__(self, tall, tail):
        self.tall, self.tail = tall, tail
        self.total = SLOTS * tall + tail

    def lone(self):
        return pl.ds(LONE * self.tall, self.tail)

    def tile(self, u, d):
        i = u * WAYS + d
        return pl.ds(i * self.tall + (self.tail if i >= LONE else 0), self.tall)

    def pair(self, u):
        return pl.ds(u * WAYS * self.tall, WAYS * self.tall + (self.tail if u == UNITS - 1 else 0))

    def half(self, u, d, lone=True):
        i = u * WAYS + d
        more = self.tail if (u == UNITS - 1 and lone) else 0
        start = i * self.tall + (self.tail if (i >= LONE and not lone) else 0)
        return pl.ds(start, self.tall + more)


def reduce_kernel(
    chips, n_seq, seq_len,
    len_ref, x_hbm, w_hbm, ag, ag_pair,
    x_raw, xc, wbuf, part, part_in, tx_hi, tx_lo, rx_hi, rx_lo,
    x_sem, w_sem, pp_send, pp_recv, hi_send, hi_recv, lo_send, lo_recv, ag_send, ag_recv, ap_send, ap_recv,
):
    me = lax.axis_index("tp")
    z, core = me // CORES, lax.rem(me, CORES)
    nxt = lax.rem(z + 1, chips) * CORES + core
    prv = lax.rem(z + chips - 1, chips) * CORES + core
    mate = z * CORES + (1 - core)
    body_rows = (n_seq - 1) * seq_len
    far = chips // 2
    last = UNITS - 1
    wide, packed, low = Rows(body_rows, 8), Rows(body_rows, 16), Rows(body_rows // 2, 0)

    def place(t, side):
        return jnp.where(t == 0, 0, jnp.where(t == far, 2 * far - 1, 2 * t - 1 + side))

    def w_copy(t, u, side):
        chunk = lax.rem(z + chips + (t - far if side == 0 else far - t), chips)
        col = pl.multiple_of((chunk * UNITS + u) * BLOCK, BLOCK)
        b = u * WAYS + side
        return pltpu.make_async_copy(w_hbm.at[:, pl.ds(col, BLOCK)], wbuf.at[b], w_sem.at[b])

    x_copy = pltpu.make_async_copy(x_hbm, x_raw, x_sem)
    x_copy.start()
    w_copy(0, 0, 0).start()

    barrier = pltpu.get_barrier_semaphore()
    for peer in (mate, nxt, prv):
        pl.semaphore_signal(barrier, inc=1, device_id={"tp": peer}, device_id_type=MESH)

    single = first_single(len_ref, n_seq)
    x_copy.wait()
    for u in range(1, UNITS):
        w_copy(0, u, 0).start()
    for u in range(UNITS):
        w_copy(1, u, 1).start()

    def x_rows(slot, count):
        return x_raw[slot * seq_len:slot * seq_len + count, :]

    for p in range(n_seq - 1):
        xc[p * seq_len:(p + 1) * seq_len, :] = jnp.where(single <= p, x_rows(p + 1, seq_len), x_rows(p, seq_len))
    lone = x_rows(n_seq - 1, 16)
    for s in range(n_seq - 1):
        lone = jnp.where(single == s, x_rows(s, 16), lone)
    xc[body_rows:body_rows + 16, :] = lone
    pl.semaphore_wait(barrier, 3)

    def pp_copy(t, u, side):
        q = place(t, side)
        return pltpu.make_async_remote_copy(
            src_ref=part.at[1 - core, q, wide.pair(u)], dst_ref=part_in.at[q, wide.pair(u)],
            send_sem=pp_send.at[q, u], recv_sem=pp_recv.at[q, u], device_id={"tp": mate}, device_id_type=MESH)

    def rs_copies(t, u, side, far_end):
        peer = prv if side == 0 else nxt
        copies = []
        for tx, rx, ss, rs, rows in ((tx_hi, rx_hi, hi_send, hi_recv, packed), (tx_lo, rx_lo, lo_send, lo_recv, low)):
            where = rows.half(u, side) if far_end else rows.pair(u)
            copies.append(pltpu.make_async_remote_copy(
                src_ref=tx.at[side, t, where], dst_ref=rx.at[side, t, where],
                send_sem=ss.at[side, t, u], recv_sem=rs.at[side, t, u], device_id={"tp": peer}, device_id_type=MESH))
        return copies

    def ag_where(u, way, half):
        return packed.half(u, way, lone=way == 0) if half else packed.pair(u)

    def slot_of(h, way):
        return h if way == 0 else lax.rem(2 * far - h, 2 * far)

    def ag_copy(h, u, way, half):
        where = ag_where(u, way, half)
        return pltpu.make_async_remote_copy(
            src_ref=ag.at[slot_of(h, way), where], dst_ref=ag.at[slot_of(h + 1, way), where],
            send_sem=ag_send.at[way, h, u], recv_sem=ag_recv.at[way, h, u],
            device_id={"tp": nxt if way == 0 else prv}, device_id_type=MESH)

    def ap_copy(h, u, way, half=False):
        where = ag_where(u, way, half)
        return pltpu.make_async_remote_copy(
            src_ref=ag.at[slot_of(h, way), where], dst_ref=ag_pair.at[slot_of(h, way), where],
            send_sem=ap_send.at[way, h, u], recv_sem=ap_recv.at[way, h, u], device_id={"tp": mate}, device_id_type=MESH)

    def compute(t, u, side):
        q = place(t, side)
        w_copy(t, u, side).wait()
        prod = jnp.dot(xc[...], wbuf[u * WAYS + side], preferred_element_type=jnp.float32)
        for d in range(WAYS):
            i = u * WAYS + d
            for half in range(CORES):
                cols = slice((d * CORES + half) * LANES, (d * CORES + half + 1) * LANES)
                part[half, q, wide.tile(u, d), :] = prod[:body_rows, cols]
                tile = LONE * body_rows
                if i == 0:
                    part[half, q, tile:tile + 8, :] = prod[body_rows:body_rows + 8, cols]
                else:
                    part[half, q, tile + i:tile + i + 1, :] = prod[body_rows:body_rows + 1, cols]
        pp_copy(t, u, side).start()

        @pl.when(t < (far if side == 0 else far - 1))
        def _():
            w_copy(t + 1, u, side).start()

    def ring(t, u, side):
        q = place(t, side)
        parity = lax.rem(lax.broadcasted_iota(jnp.int32, (8, LANES), 0), WAYS)

        def here(where):
            return part[core, q, where, :] + part_in[q, where, :]

        def arrived(side_, d):
            return join_sum(rx_hi[side_, t - 1, packed.tile(u, d), :], rx_lo[side_, t - 1, low.tile(u, d), :])

        def arrived_lone(side_):
            return join_lone(rx_hi[side_, t - 1, packed.lone(), :])

        def put(side_, d, total):
            tx_hi[side_, t, packed.tile(u, d), :], tx_lo[side_, t, low.tile(u, d), :] = split_sum(total, body_rows)

        def put_lone(side_, total):
            tx_hi[side_, t, packed.lone(), :] = split_lone(total)

        if side == 0:
            @pl.when(t == 0)
            def _():
                pp_copy(t, u, side).wait_recv()
                for d in range(WAYS):
                    put(d, d, here(wide.tile(u, d)))
                    if u == last:
                        put_lone(d, here(wide.lone()))
                    for copy in rs_copies(0, u, d, True):
                        copy.start()

        @pl.when(t == 1)
        def _():
            pp_copy(t, u, side).wait_recv()
            put(side, 1 - side, here(wide.tile(u, 1 - side)))
            for copy in rs_copies(0, u, side, True):
                copy.wait_recv()
            put(side, side, here(wide.tile(u, side)) + arrived(side, side))
            if u == last:
                put_lone(side, here(wide.lone()) + jnp.where(parity == side, arrived_lone(side), 0.0))
            for copy in rs_copies(1, u, side, False):
                copy.start()

        @pl.when(jnp.logical_and(t > 1, t < far))
        def _():
            pp_copy(t, u, side).wait_recv()
            for copy in rs_copies(t - 1, u, side, False):
                copy.wait_recv()
            for d in range(WAYS):
                put(side, d, here(wide.tile(u, d)) + arrived(side, d))
            if u == last:
                put_lone(side, here(wide.lone()) + arrived_lone(side))
            for copy in rs_copies(t, u, side, False):
                copy.start()

        if side == 0:
            @pl.when(t == far)
            def _():
                pp_copy(t, u, side).wait_recv()
                for way in range(WAYS):
                    for copy in rs_copies(t - 1, u, way, False):
                        copy.wait_recv()
                for d in range(WAYS):
                    total = (here(wide.tile(u, d)) + arrived(0, d)) + arrived(1, d)
                    ag[0, packed.tile(u, d), :] = total.astype(jnp.bfloat16)
                if u == last:
                    total = (here(wide.lone()) + arrived_lone(0)) + arrived_lone(1)
                    ag[0, packed.lone(), :] = jnp.concatenate([total, total], axis=0).astype(jnp.bfloat16)
                for way in range(WAYS):
                    ag_copy(0, u, way, False).start()
                ap_copy(0, u, 0).start()

    turns = [(u, side) for u in range(UNITS) for side in range(WAYS)]

    @pl.loop(0, far + 1)
    def _(t):
        for i, (u, side) in enumerate(turns):
            if side == 0:
                compute(t, u, side)
            else:
                @pl.when(jnp.logical_and(t > 0, t < far))
                def _():
                    compute(t, u, side)
            if i >= 2:
                ring(t, *turns[i - 2])
            else:
                @pl.when(t > 0)
                def _():
                    ring(t - 1, *turns[i - 2])

    ring(jnp.int32(far), *turns[-2])

    def pass_on(h, half):
        for u in range(UNITS):
            for way in range(WAYS):
                ag_copy(h - 1, u, way, False).wait_recv()
                ag_copy(h, u, way, half).start()
                ap_copy(h, u, way).start()

    @pl.loop(1, far - 1)
    def _(h):
        pass_on(h, False)

    pass_on(far - 1, True)
    for u in range(UNITS):
        for way in range(WAYS):
            ag_copy(far - 1, u, way, True).wait_recv()
            ap_copy(far, u, way, True).start()

    for u in range(UNITS):
        ap_copy(0, u, 0).wait()
        for side in range(WAYS):
            for copy in rs_copies(0, u, side, True):
                copy.wait_send()
            ag_copy(far - 1, u, side, True).wait_send()
            ap_copy(far, u, side, True).wait()

    @pl.loop(0, 2 * far)
    def _(q):
        for u in range(UNITS):
            pltpu.make_async_remote_copy(
                src_ref=part.at[1 - core, q, wide.pair(u)], dst_ref=part_in.at[q, wide.pair(u)],
                send_sem=pp_send.at[q, u], recv_sem=pp_recv.at[q, u], device_id={"tp": mate}, device_id_type=MESH).wait_send()

    @pl.loop(1, far)
    def _(t):
        for u in range(UNITS):
            for side in range(WAYS):
                for copy in rs_copies(t, u, side, False):
                    copy.wait_send()
                ag_copy(t - 1, u, side, False).wait_send()
                ap_copy(t, u, side).wait()


def expand_kernel(chips, n_seq, seq_len, len_ref, ag, ag_pair, o_hbm, keep, alone, stage, sems):
    me = lax.axis_index("tp")
    z, core = me // CORES, lax.rem(me, CORES)
    body_rows = (n_seq - 1) * seq_len
    packed = Rows(body_rows, 16)
    single = first_single(len_ref, n_seq)
    row = lax.broadcasted_iota(jnp.int32, (seq_len, LANES), 0)
    for s in range(n_seq):
        many = jnp.where(single == s, 0, len_ref[s])
        one = jnp.where(single == s, 1, 0)
        keep[s * seq_len:(s + 1) * seq_len, :] = jnp.where(row < many, 1.0, 0.0).astype(jnp.bfloat16)
        alone[s * 16:(s + 1) * 16, :] = jnp.where(row[:16] < one, 1.0, 0.0).astype(jnp.bfloat16)
    zero = jnp.bfloat16(0)

    def out_copy(slot):
        cols = pl.ds(pl.multiple_of(lax.rem(z + chips - slot, chips) * (UNITS * BLOCK), UNITS * BLOCK), UNITS * BLOCK)
        return pltpu.make_async_copy(stage.at[slot], o_hbm.at[:, cols], sems.at[slot])

    @pl.loop(0, chips)
    def _(slot):
        for near, ref in enumerate((ag, ag_pair)):
            side = core if near == 0 else 1 - core
            tail = ref[slot, packed.lone(), :].astype(jnp.float32)
            for i in range(SLOTS):
                cols = pl.ds(pl.multiple_of((i * CORES + side) * LANES, LANES), LANES)
                lone = jnp.broadcast_to(tail[i:i + 1, :], (16, LANES)).astype(jnp.bfloat16)
                top = packed.tile(i // WAYS, i % WAYS).start
                for s in range(n_seq):
                    pos = jnp.minimum(s - (single < s).astype(jnp.int32), n_seq - 2)
                    rows = ref[slot, pl.ds(pl.multiple_of(top + pos * seq_len, 16), seq_len), :]
                    mask = keep[s * seq_len:(s + 1) * seq_len, :]
                    first = jnp.where(alone[s * 16:(s + 1) * 16, :] > zero, lone, zero)
                    base = s * seq_len
                    stage[slot, base:base + 16, cols] = jnp.where(mask[:16] > zero, rows[:16], first)
                    stage[slot, base + 16:base + seq_len, cols] = jnp.where(mask[16:] > zero, rows[16:], zero)
        out_copy(slot).start()

    @pl.loop(0, chips)
    def _(slot):
        out_copy(slot).wait()


def solution(mesh):
    chips = mesh.shape["tp"] // CORES

    def local_part(x_loc, w_loc, lengths):
        tokens, depth = x_loc.shape
        columns = w_loc.shape[1]
        n_seq = lengths.shape[0]
        seq_len = tokens // n_seq
        body_rows = (n_seq - 1) * seq_len
        far = chips // 2
        assert columns == chips * UNITS * BLOCK and chips == 2 * far and far >= 3
        wide, packed, low = Rows(body_rows, 8), Rows(body_rows, 16), Rows(body_rows // 2, 0)
        dma = pltpu.SemaphoreType.DMA
        held = pltpu.VMEM((chips, packed.total, LANES), jnp.bfloat16)
        vmem = pl.BlockSpec(memory_space=pltpu.VMEM)
        smem = pl.BlockSpec(memory_space=pltpu.SMEM)
        hbm = pl.BlockSpec(memory_space=pl.ANY)
        high = pltpu.VMEM((WAYS, far, packed.total, LANES), jnp.bfloat16)
        lows = pltpu.VMEM((WAYS, far, low.total, LANES), jnp.int16)
        hops = dma((WAYS, far, UNITS))
        near, others = pl.pallas_call(
            functools.partial(reduce_kernel, chips, n_seq, seq_len),
            out_shape=(held, held),
            in_specs=[smem, hbm, hbm],
            out_specs=(vmem, vmem),
            scratch_shapes=[
                pltpu.VMEM((tokens, depth), jnp.bfloat16),
                pltpu.VMEM((body_rows + 16, depth), jnp.bfloat16),
                pltpu.VMEM((SLOTS, depth, BLOCK), jnp.bfloat16),
                pltpu.VMEM((CORES, chips, wide.total, LANES), jnp.float32),
                pltpu.VMEM((chips, wide.total, LANES), jnp.float32),
                high, lows, high, lows,
                dma,
                dma((SLOTS,)),
                dma((chips, UNITS)), dma((chips, UNITS)),
                hops, hops, hops, hops, hops, hops,
                dma((WAYS, far + 1, UNITS)), dma((WAYS, far + 1, UNITS)),
            ],
            compiler_params=pltpu.CompilerParams(
                collective_id=0, has_side_effects=True, vmem_limit_bytes=52 * 1024 * 1024),
            name="reduce_gather",
        )(lengths, x_loc, w_loc)
        return pl.pallas_call(
            functools.partial(expand_kernel, chips, n_seq, seq_len),
            out_shape=jax.ShapeDtypeStruct((tokens, columns), jnp.bfloat16),
            in_specs=[smem, vmem, vmem],
            out_specs=hbm,
            scratch_shapes=[
                pltpu.VMEM((tokens, LANES), jnp.bfloat16),
                pltpu.VMEM((n_seq * 16, LANES), jnp.bfloat16),
                pltpu.VMEM((chips, tokens, UNITS * BLOCK), jnp.bfloat16),
                dma((chips,)),
            ],
            compiler_params=pltpu.CompilerParams(vmem_limit_bytes=32 * 1024 * 1024),
            name="expand_rows",
        )(lengths, near, others)

    return jax.shard_map(local_part, mesh=mesh, in_specs=(P("data", "tp"), P("tp", None), P("data")), out_specs=P("data", None), check_vma=False)
```

time: 181 us -> 80.9 us (0.45)
  waiting for transfers between devices: 123 us -> 0 us
  Pallas kernels: 0 us -> 80.8 us
  matrix products: 33.2 us -> 0 us
  between operations: 13.4 us -> 0.02 us
  local copies, waits for them, and re-layouts: 8.23 us -> 0.01 us
  other arithmetic: 2.06 us -> 0 us
    pallas_call x0 -> x2, Pallas kernels: none -> 80.8 us  [the longest x1 77.2 us: local_part(): pl.pallas_call(functools.partial(reduce_kernel, chips, n_seq, seq_len), o...]
    reduce_scatter x1 -> x0, waiting for transfers between devices: 79.4 us -> none  [local_part(): own_rows = lax.psum_scatter(part_sum, 'tp', scatter_dimension=0, tiled=True)]
    all_gather x1 -> x0, waiting for transfers between devices: 43.7 us -> none  [local_part(): return lax.all_gather(own_out, 'tp', axis=0, tiled=True)]
    dot_general x1 -> x0, matrix products: 33.2 us -> none  [local_part(): part_sum = jnp.dot(x_loc, w_loc, preferred_element_type=jnp.float32)]
    unnamed x5 -> x2, local copies, waits for them, and re-layouts: 8.07 us -> 0.01 us
    convert_element_type x1 -> x0, other arithmetic: 1.99 us -> none  [local_part(): own_out = jnp.where(own_valid[:, None], own_rows, 0.0).astype(jnp.bfloat16)]
  transfers between devices with their start and end apart: 2 -> 0, of which waited for: 2 -> 0; matrix products, arithmetic and copies ran while one was open for 0% -> 0% of each run, Pallas kernels for 0% -> 0%
where the time goes in v4:
time: 80.9 us
  Pallas kernels  80.8 us (100%)
    pallas_call x1, Pallas kernels, local_part(): pl.pallas_call(functools.partial(reduce_kernel, chips, n_seq, seq_len), o...  77.2 us
    pallas_call x1, Pallas kernels, local_part(): pl.pallas_call(functools.partial(expand_kernel, chips, n_seq, seq_len), o...  3.63 us

profile of v4, /device:TPU:21, one launch (start us, length us, event | category | flops | bytes accessed | tf_op | source)
XLA Modules:
  0.0 80.9 jit_solution(8713982557912063315)
XLA Ops:
  0.0 0.0 copy-start
  0.0 77.2 %reduce_gather.1 = (bf16[8,1168,128]{2,1,0:T(8,128)(2,1)S(1)}, bf16[8,1168,128]{2,1,0:T(8,128)(2,1)S(1)}) custom-call(s32[4]{0:T(128)} %len_ref.3, bf16[256,3072]{1,0:T(8,128)(2,1)} %x_hbm.1, bf16[3072,12288]{1,0:T(8,128)(2,1)} %w_hbm.1), custom_call_target="tpu_custom_call" | custom-call | tf_op jit(solution)/shard_map/reduce_gather/pallas_call | solution.py:377
  77.2 0.0 copy-done
  77.2 3.6 %expand_rows.1 = bf16[256,12288]{1,0:T(8,128)(2,1)} custom-call(s32[4]{0:T(128)S(1)} %copy-done, bf16[8,1168,128]{2,1,0:T(8,128)(2,1)S(1)} %get-tuple-element.7.ag, bf16[8,1168,128]{2,1,0:T(8,128)(2,1)S(1)} %get-tuple-element.8.ag_pair), custom_call_target="tpu_custom_call" | custom-call | tf_op jit(solution)/shard_map/expand_rows/pallas_call | solution.py:399
Async XLA Ops:
  0.0 77.2 %copy-start = (s32[4]{0:T(128)S(1)}, s32[4]{0:T(128)}, u32[]{:S(2)}) copy-start(s32[4]{0:T(128)} %len_ref.3) | copy-start | bytes 52

commit v5 on v4

--- a/solution.py
+++ b/solution.py
@@ -75,8 +75,8 @@
 
 def reduce_kernel(
     chips, n_seq, seq_len,
-    len_ref, x_hbm, w_hbm, ag, ag_pair,
-    x_raw, xc, wbuf, part, part_in, tx_hi, tx_lo, rx_hi, rx_lo,
+    len_ref, x_hbm, w_hbm, y_ref,
+    x_raw, xc, wbuf, part, part_in, tx_hi, tx_lo, rx_hi, rx_lo, ag, ag_pair, keep, alone,
     x_sem, w_sem, pp_send, pp_recv, hi_send, hi_recv, lo_send, lo_recv, ag_send, ag_recv, ap_send, ap_recv,
 ):
     me = lax.axis_index("tp")
@@ -108,10 +108,7 @@
 
     single = first_single(len_ref, n_seq)
     x_copy.wait()
-    for u in range(1, UNITS):
-        w_copy(0, u, 0).start()
-    for u in range(UNITS):
-        w_copy(1, u, 1).start()
+    w_copy(0, 1, 0).start()
 
     def x_rows(slot, count):
         return x_raw[slot * seq_len:slot * seq_len + count, :]
@@ -122,7 +119,40 @@
     for s in range(n_seq - 1):
         lone = jnp.where(single == s, x_rows(s, 16), lone)
     xc[body_rows:body_rows + 16, :] = lone
+    row = lax.broadcasted_iota(jnp.int32, (seq_len, LANES), 0)
+    zero = jnp.bfloat16(0)
+    for s in range(n_seq):
+        many = jnp.where(single == s, 0, len_ref[s])
+        one = jnp.where(single == s, 1, 0)
+        keep[s * seq_len:(s + 1) * seq_len, :] = jnp.where(row < many, 1.0, 0.0).astype(jnp.bfloat16)
+        alone[s * 16:(s + 1) * 16, :] = jnp.where(row[:16] < one, 1.0, 0.0).astype(jnp.bfloat16)
     pl.semaphore_wait(barrier, 3)
+
+    def out_cols(slot, i, owner):
+        chunk = lax.rem(z + chips - slot, chips)
+        return pl.ds(pl.multiple_of(((chunk * SLOTS + i) * CORES + owner) * LANES, LANES), LANES)
+
+    def expand(slot, u, ways, ref, owner):
+        for d in ways:
+            cols = out_cols(slot, u * WAYS + d, owner)
+            top = packed.tile(u, d).start
+            block = [ref[slot, top + p * seq_len:top + (p + 1) * seq_len, :] for p in range(n_seq - 1)]
+            for s in range(n_seq):
+                if s == 0 or s == n_seq - 1:
+                    rows = block[min(s, n_seq - 2)]
+                else:
+                    rows = jnp.where(single < s, block[s - 1], block[s])
+                mask = keep[s * seq_len:(s + 1) * seq_len, :]
+                y_ref[s * seq_len:(s + 1) * seq_len, cols] = jnp.where(mask > zero, rows, zero)
+
+    def expand_lone(slot, ref, owner):
+        tail = ref[slot, packed.lone(), :].astype(jnp.float32)
+        for i in range(SLOTS):
+            cols = out_cols(slot, i, owner)
+            value = jnp.broadcast_to(tail[i:i + 1, :], (16, LANES)).astype(jnp.bfloat16)
+            for s in range(n_seq):
+                rows = slice(s * seq_len, s * seq_len + 16)
+                y_ref[rows, cols] = jnp.where(alone[s * 16:(s + 1) * 16, :] > zero, value, y_ref[rows, cols])
 
     def pp_copy(t, u, side):
         q = place(t, side)
@@ -162,6 +192,14 @@
     def compute(t, u, side):
         q = place(t, side)
         w_copy(t, u, side).wait()
+        if u == 0 and side == 0:
+            @pl.when(t == 0)
+            def _():
+                for v in range(2, UNITS):
+                    w_copy(0, v, 0).start()
+                for v in range(UNITS):
+                    w_copy(1, v, 1).start()
+
         prod = jnp.dot(xc[...], wbuf[u * WAYS + side], preferred_element_type=jnp.float32)
         for d in range(WAYS):
             i = u * WAYS + d
@@ -249,6 +287,9 @@
                 for way in range(WAYS):
                     ag_copy(0, u, way, False).start()
                 ap_copy(0, u, 0).start()
+                expand(0, u, range(WAYS), ag, core)
+                if u == last:
+                    expand_lone(0, ag, core)
 
     turns = [(u, side) for u in range(UNITS) for side in range(WAYS)]
 
@@ -270,30 +311,43 @@
 
     ring(jnp.int32(far), *turns[-2])
 
-    def pass_on(h, half):
+    def mates(h, u, way):
+        ap_copy(h, u, way).wait_recv()
+        expand(slot_of(h, way), u, range(WAYS), ag_pair, 1 - core)
+        if u == last:
+            expand_lone(slot_of(h, way), ag_pair, 1 - core)
+
+    for h in range(1, far):
         for u in range(UNITS):
             for way in range(WAYS):
                 ag_copy(h - 1, u, way, False).wait_recv()
-                ag_copy(h, u, way, half).start()
+                ag_copy(h, u, way, h == far - 1).start()
                 ap_copy(h, u, way).start()
-
-    @pl.loop(1, far - 1)
-    def _(h):
-        pass_on(h, False)
-
-    pass_on(far - 1, True)
+                expand(slot_of(h, way), u, range(WAYS), ag, core)
+                if u == last:
+                    expand_lone(slot_of(h, way), ag, core)
+                if h > 1 or way == 0:
+                    mates(h - 1, u, way)
     for u in range(UNITS):
         for way in range(WAYS):
             ag_copy(far - 1, u, way, True).wait_recv()
             ap_copy(far, u, way, True).start()
-
+            expand(far, u, (way,), ag, core)
+            mates(far - 1, u, way)
+    expand_lone(far, ag, core)
     for u in range(UNITS):
-        ap_copy(0, u, 0).wait()
+        for way in range(WAYS):
+            ap_copy(far, u, way, True).wait_recv()
+            expand(far, u, (way,), ag_pair, 1 - core)
+    expand_lone(far, ag_pair, 1 - core)
+
+    for u in range(UNITS):
+        ap_copy(0, u, 0).wait_send()
         for side in range(WAYS):
             for copy in rs_copies(0, u, side, True):
                 copy.wait_send()
             ag_copy(far - 1, u, side, True).wait_send()
-            ap_copy(far, u, side, True).wait()
+            ap_copy(far, u, side, True).wait_send()
 
     @pl.loop(0, 2 * far)
     def _(q):
@@ -309,49 +363,7 @@
                 for copy in rs_copies(t, u, side, False):
                     copy.wait_send()
                 ag_copy(t - 1, u, side, False).wait_send()
-                ap_copy(t, u, side).wait()
-
-
-def expand_kernel(chips, n_seq, seq_len, len_ref, ag, ag_pair, o_hbm, keep, alone, stage, sems):
-    me = lax.axis_index("tp")
-    z, core = me // CORES, lax.rem(me, CORES)
-    body_rows = (n_seq - 1) * seq_len
-    packed = Rows(body_rows, 16)
-    single = first_single(len_ref, n_seq)
-    row = lax.broadcasted_iota(jnp.int32, (seq_len, LANES), 0)
-    for s in range(n_seq):
-        many = jnp.where(single == s, 0, len_ref[s])
-        one = jnp.where(single == s, 1, 0)
-        keep[s * seq_len:(s + 1) * seq_len, :] = jnp.where(row < many, 1.0, 0.0).astype(jnp.bfloat16)
-        alone[s * 16:(s + 1) * 16, :] = jnp.where(row[:16] < one, 1.0, 0.0).astype(jnp.bfloat16)
-    zero = jnp.bfloat16(0)
-
-    def out_copy(slot):
-        cols = pl.ds(pl.multiple_of(lax.rem(z + chips - slot, chips) * (UNITS * BLOCK), UNITS * BLOCK), UNITS * BLOCK)
-        return pltpu.make_async_copy(stage.at[slot], o_hbm.at[:, cols], sems.at[slot])
-
-    @pl.loop(0, chips)
-    def _(slot):
-        for near, ref in enumerate((ag, ag_pair)):
-            side = core if near == 0 else 1 - core
-            tail = ref[slot, packed.lone(), :].astype(jnp.float32)
-            for i in range(SLOTS):
-                cols = pl.ds(pl.multiple_of((i * CORES + side) * LANES, LANES), LANES)
-                lone = jnp.broadcast_to(tail[i:i + 1, :], (16, LANES)).astype(jnp.bfloat16)
-                top = packed.tile(i // WAYS, i % WAYS).start
-                for s in range(n_seq):
-                    pos = jnp.minimum(s - (single < s).astype(jnp.int32), n_seq - 2)
-                    rows = ref[slot, pl.ds(pl.multiple_of(top + pos * seq_len, 16), seq_len), :]
-                    mask = keep[s * seq_len:(s + 1) * seq_len, :]
-                    first = jnp.where(alone[s * 16:(s + 1) * 16, :] > zero, lone, zero)
-                    base = s * seq_len
-                    stage[slot, base:base + 16, cols] = jnp.where(mask[:16] > zero, rows[:16], first)
-                    stage[slot, base + 16:base + seq_len, cols] = jnp.where(mask[16:] > zero, rows[16:], zero)
-        out_copy(slot).start()
-
-    @pl.loop(0, chips)
-    def _(slot):
-        out_copy(slot).wait()
+                ap_copy(t, u, side).wait_send()
 
 
 def solution(mesh):
@@ -374,18 +386,20 @@
         high = pltpu.VMEM((WAYS, far, packed.total, LANES), jnp.bfloat16)
         lows = pltpu.VMEM((WAYS, far, low.total, LANES), jnp.int16)
         hops = dma((WAYS, far, UNITS))
-        near, others = pl.pallas_call(
+        return pl.pallas_call(
             functools.partial(reduce_kernel, chips, n_seq, seq_len),
-            out_shape=(held, held),
+            out_shape=pltpu.VMEM((tokens, columns), jnp.bfloat16),
             in_specs=[smem, hbm, hbm],
-            out_specs=(vmem, vmem),
+            out_specs=vmem,
             scratch_shapes=[
                 pltpu.VMEM((tokens, depth), jnp.bfloat16),
                 pltpu.VMEM((body_rows + 16, depth), jnp.bfloat16),
                 pltpu.VMEM((SLOTS, depth, BLOCK), jnp.bfloat16),
                 pltpu.VMEM((CORES, chips, wide.total, LANES), jnp.float32),
                 pltpu.VMEM((chips, wide.total, LANES), jnp.float32),
-                high, lows, high, lows,
+                high, lows, high, lows, held, held,
+                pltpu.VMEM((tokens, LANES), jnp.bfloat16),
+                pltpu.VMEM((n_seq * 16, LANES), jnp.bfloat16),
                 dma,
                 dma((SLOTS,)),
                 dma((chips, UNITS)), dma((chips, UNITS)),
@@ -393,22 +407,8 @@
                 dma((WAYS, far + 1, UNITS)), dma((WAYS, far + 1, UNITS)),
             ],
             compiler_params=pltpu.CompilerParams(
-                collective_id=0, has_side_effects=True, vmem_limit_bytes=52 * 1024 * 1024),
+                collective_id=0, has_side_effects=True, vmem_limit_bytes=54 * 1024 * 1024),
             name="reduce_gather",
         )(lengths, x_loc, w_loc)
-        return pl.pallas_call(
-            functools.partial(expand_kernel, chips, n_seq, seq_len),
-            out_shape=jax.ShapeDtypeStruct((tokens, columns), jnp.bfloat16),
-            in_specs=[smem, vmem, vmem],
-            out_specs=hbm,
-            scratch_shapes=[
-                pltpu.VMEM((tokens, LANES), jnp.bfloat16),
-                pltpu.VMEM((n_seq * 16, LANES), jnp.bfloat16),
-                pltpu.VMEM((chips, tokens, UNITS * BLOCK), jnp.bfloat16),
-                dma((chips,)),
-            ],
-            compiler_params=pltpu.CompilerParams(vmem_limit_bytes=32 * 1024 * 1024),
-            name="expand_rows",
-        )(lengths, near, others)
 
     return jax.shard_map(local_part, mesh=mesh, in_specs=(P("data", "tp"), P("tp", None), P("data")), out_specs=P("data", None), check_vma=False)

time: 80.9 us -> 80 us (0.989)
  Pallas kernels: 80.8 us -> 77.2 us
  local copies, waits for them, and re-layouts: 0.01 us -> 2.71 us
    pallas_call x1 -> x0, Pallas kernels: 3.63 us -> none  [local_part(): pl.pallas_call(functools.partial(expand_kernel, chips, n_seq, seq_len), o...]
    unnamed x2 -> x1, local copies, waits for them, and re-layouts: 0.01 us -> 2.71 us
where the time goes in v5:
time: 80 us; the launch traced here: 79.9 us
  Pallas kernels  77.2 us (96%)
  local copies, waits for them, and re-layouts  2.71 us (3%)
    pallas_call x1, Pallas kernels, local_part(): pl.pallas_call(functools.partial(reduce_kernel, chips, n_seq, seq_len), o...  77.2 us
    unnamed x1, local copies, waits for them, and re-layouts  2.71 us

profile of v5, /device:TPU:21, one launch (start us, length us, event | category | flops | bytes accessed | tf_op | source)
XLA Modules:
  0.0 79.9 jit_solution(8000674523115832144)
XLA Ops:
  0.0 77.2 %reduce_gather.1 = bf16[256,12288]{1,0:T(8,128)(2,1)S(1)} custom-call(s32[4]{0:T(128)} %len_ref.1, bf16[256,3072]{1,0:T(8,128)(2,1)} %x_hbm.1, bf16[3072,12288]{1,0:T(8,128)(2,1)} %w_hbm.1), custom_call_target="tpu_custom_call" | custom-call | tf_op jit(solution)/shard_map/reduce_gather/pallas_call | solution.py:389
  77.2 2.7 %copy.5 = bf16[256,12288]{1,0:T(8,128)(2,1)} copy(bf16[256,12288]{1,0:T(8,128)(2,1)S(1)} %reduce_gather.1) | data formatting | bytes 12582912

commit v6 on v5

--- a/solution.py
+++ b/solution.py
@@ -15,7 +15,9 @@
 SLOTS = UNITS * WAYS
 BLOCK = CORES * WAYS * LANES
 LONE = UNITS * WAYS - 1
-STEPS = 127 * 256
+LOWS = 3
+LEVELS = 39
+STEPS = (LEVELS // 2) * 256
 
 
 def first_single(len_ref, n_seq):
@@ -29,14 +31,17 @@
     high = total.astype(jnp.bfloat16)
     wide = high.astype(jnp.float32)
     left = jnp.round((total - wide) / jnp.where(wide == 0.0, 1.0, wide) * STEPS)
-    low = left[:rows // 2] * 256.0 + left[rows // 2:]
+    third = rows // LOWS
+    low = (left[:third] * LEVELS + left[third:2 * third]) * LEVELS + left[2 * third:]
     return high, low.astype(jnp.int32).astype(jnp.int16)
 
 
 def join_sum(high, low):
-    pair = low.astype(jnp.int32).astype(jnp.float32)
-    first = jnp.round(pair * (1.0 / 256.0))
-    left = jnp.concatenate([first, pair - first * 256.0], axis=0)
+    code = low.astype(jnp.int32).astype(jnp.float32)
+    first = jnp.round(code * (1.0 / LEVELS ** 2))
+    rest = code - first * LEVELS ** 2
+    second = jnp.round(rest * (1.0 / LEVELS))
+    left = jnp.concatenate([first, second, rest - second * LEVELS], axis=0)
     wide = high.astype(jnp.float32)
     return wide + wide * (left * (1.0 / STEPS))
 
@@ -87,7 +92,7 @@
     body_rows = (n_seq - 1) * seq_len
     far = chips // 2
     last = UNITS - 1
-    wide, packed, low = Rows(body_rows, 8), Rows(body_rows, 16), Rows(body_rows // 2, 0)
+    wide, packed, low = Rows(body_rows, 8), Rows(body_rows, 16), Rows(body_rows // LOWS, 0)
 
     def place(t, side):
         return jnp.where(t == 0, 0, jnp.where(t == far, 2 * far - 1, 2 * t - 1 + side))
@@ -377,7 +382,7 @@
         body_rows = (n_seq - 1) * seq_len
         far = chips // 2
         assert columns == chips * UNITS * BLOCK and chips == 2 * far and far >= 3
-        wide, packed, low = Rows(body_rows, 8), Rows(body_rows, 16), Rows(body_rows // 2, 0)
+        wide, packed, low = Rows(body_rows, 8), Rows(body_rows, 16), Rows(body_rows // LOWS, 0)
         dma = pltpu.SemaphoreType.DMA
         held = pltpu.VMEM((chips, packed.total, LANES), jnp.bfloat16)
         vmem = pl.BlockSpec(memory_space=pltpu.VMEM)

time: 80 us -> 76.9 us (0.961)
  Pallas kernels: 77.2 us -> 74.1 us
    pallas_call x1, Pallas kernels: 77.2 us -> 74.1 us  [local_part(): pl.pallas_call(functools.partial(reduce_kernel, chips, n_seq, seq_len), o...]
where the time goes in v6:
time: 76.9 us; the launch traced here: 76.8 us
  Pallas kernels  74.1 us (96%)
  local copies, waits for them, and re-layouts  2.71 us (4%)
    pallas_call x1, Pallas kernels, local_part(): pl.pallas_call(functools.partial(reduce_kernel, chips, n_seq, seq_len), o...  74.1 us
    unnamed x1, local copies, waits for them, and re-layouts  2.71 us

profile of v6, /device:TPU:21, one launch (start us, length us, event | category | flops | bytes accessed | tf_op | source)
XLA Modules:
  0.0 76.8 jit_solution(9727857196481511662)
XLA Ops:
  0.0 74.1 %reduce_gather.1 = bf16[256,12288]{1,0:T(8,128)(2,1)S(1)} custom-call(s32[4]{0:T(128)} %len_ref.1, bf16[256,3072]{1,0:T(8,128)(2,1)} %x_hbm.1, bf16[3072,12288]{1,0:T(8,128)(2,1)} %w_hbm.1), custom_call_target="tpu_custom_call" | custom-call | tf_op jit(solution)/shard_map/reduce_gather/pallas_call | solution.py:394
  74.1 2.7 %copy.5 = bf16[256,12288]{1,0:T(8,128)(2,1)} copy(bf16[256,12288]{1,0:T(8,128)(2,1)S(1)} %reduce_gather.1) | data formatting | bytes 12582912

commit v7 on v6

--- a/solution.py
+++ b/solution.py
@@ -13,6 +13,7 @@
 WAYS = 2
 UNITS = 3
 SLOTS = UNITS * WAYS
+AHEAD = 3
 BLOCK = CORES * WAYS * LANES
 LONE = UNITS * WAYS - 1
 LOWS = 3
@@ -97,15 +98,26 @@
     def place(t, side):
         return jnp.where(t == 0, 0, jnp.where(t == far, 2 * far - 1, 2 * t - 1 + side))
 
-    def w_copy(t, u, side):
-        chunk = lax.rem(z + chips + (t - far if side == 0 else far - t), chips)
+    blocks = chips * UNITS
+
+    def turn(t, u, side):
+        middle = UNITS + (t - 1) * SLOTS + u * WAYS + side
+        return jnp.where(t == 0, u, jnp.where(t == far, blocks - UNITS + u, middle))
+
+    def w_copy(n):
+        ends = jnp.where(n < UNITS, n, n - (blocks - UNITS))
+        inner = jnp.logical_and(n >= UNITS, n < blocks - UNITS)
+        i = jnp.where(inner, lax.rem(n + (SLOTS - UNITS), SLOTS), ends * WAYS)
+        t = jnp.where(n < UNITS, 0, (n + (SLOTS - UNITS)) // SLOTS)
+        u, side = i // WAYS, lax.rem(i, WAYS)
+        chunk = lax.rem(z + chips + jnp.where(side == 0, t - far, far - t), chips)
         col = pl.multiple_of((chunk * UNITS + u) * BLOCK, BLOCK)
-        b = u * WAYS + side
+        b = lax.rem(n, SLOTS)
         return pltpu.make_async_copy(w_hbm.at[:, pl.ds(col, BLOCK)], wbuf.at[b], w_sem.at[b])
 
     x_copy = pltpu.make_async_copy(x_hbm, x_raw, x_sem)
     x_copy.start()
-    w_copy(0, 0, 0).start()
+    w_copy(jnp.int32(0)).start()
 
     barrier = pltpu.get_barrier_semaphore()
     for peer in (mate, nxt, prv):
@@ -113,7 +125,7 @@
 
     single = first_single(len_ref, n_seq)
     x_copy.wait()
-    w_copy(0, 1, 0).start()
+    w_copy(jnp.int32(1)).start()
 
     def x_rows(slot, count):
         return x_raw[slot * seq_len:slot * seq_len + count, :]
@@ -196,16 +208,19 @@
 
     def compute(t, u, side):
         q = place(t, side)
-        w_copy(t, u, side).wait()
+        n = turn(t, u, side)
+        w_copy(n).wait()
         if u == 0 and side == 0:
             @pl.when(t == 0)
             def _():
-                for v in range(2, UNITS):
-                    w_copy(0, v, 0).start()
-                for v in range(UNITS):
-                    w_copy(1, v, 1).start()
-
-        prod = jnp.dot(xc[...], wbuf[u * WAYS + side], preferred_element_type=jnp.float32)
+                for early in range(2, AHEAD):
+                    w_copy(jnp.int32(early)).start()
+
+        @pl.when(n + AHEAD < blocks)
+        def _():
+            w_copy(n + AHEAD).start()
+
+        prod = jnp.dot(xc[...], wbuf[lax.rem(n, SLOTS)], preferred_element_type=jnp.float32)
         for d in range(WAYS):
             i = u * WAYS + d
             for half in range(CORES):
@@ -217,10 +232,6 @@
                 else:
                     part[half, q, tile + i:tile + i + 1, :] = prod[body_rows:body_rows + 1, cols]
         pp_copy(t, u, side).start()
-
-        @pl.when(t < (far if side == 0 else far - 1))
-        def _():
-            w_copy(t + 1, u, side).start()
 
     def ring(t, u, side):
         q = place(t, side)

time: 76.9 us -> 74.6 us (0.970)
  Pallas kernels: 74.1 us -> 71.8 us
    pallas_call x1, Pallas kernels: 74.1 us -> 71.8 us  [local_part(): pl.pallas_call(functools.partial(reduce_kernel, chips, n_seq, seq_len), o...]
where the time goes in v7:
time: 74.6 us; the launch traced here: 74.5 us
  Pallas kernels  71.8 us (96%)
  local copies, waits for them, and re-layouts  2.71 us (4%)
    pallas_call x1, Pallas kernels, local_part(): pl.pallas_call(functools.partial(reduce_kernel, chips, n_seq, seq_len), o...  71.8 us
    unnamed x1, local copies, waits for them, and re-layouts  2.71 us

profile of v7, /device:TPU:21, one launch (start us, length us, event | category | flops | bytes accessed | tf_op | source)
XLA Modules:
  0.0 74.5 jit_solution(12119457472703452148)
XLA Ops:
  0.0 71.8 %reduce_gather.1 = bf16[256,12288]{1,0:T(8,128)(2,1)S(1)} custom-call(s32[4]{0:T(128)} %len_ref.1, bf16[256,3072]{1,0:T(8,128)(2,1)} %x_hbm.1, bf16[3072,12288]{1,0:T(8,128)(2,1)} %w_hbm.1), custom_call_target="tpu_custom_call" | custom-call | tf_op jit(solution)/shard_map/reduce_gather/pallas_call | solution.py:405
  71.8 2.7 %copy.5 = bf16[256,12288]{1,0:T(8,128)(2,1)} copy(bf16[256,12288]{1,0:T(8,128)(2,1)S(1)} %reduce_gather.1) | data formatting | bytes 12582912

commit v8 on v7

--- a/solution.py
+++ b/solution.py
@@ -318,14 +318,26 @@
                 @pl.when(jnp.logical_and(t > 0, t < far))
                 def _():
                     compute(t, u, side)
-            if i >= 2:
-                ring(t, *turns[i - 2])
+            if i == 0:
+                @pl.when(t == 1)
+                def _():
+                    ring(jnp.int32(0), UNITS - 1, 0)
+
+                @pl.when(t > 1)
+                def _():
+                    ring(t - 1, *turns[-1])
+            elif side == 1:
+                @pl.when(t > 0)
+                def _():
+                    ring(t, u, 0)
             else:
-                @pl.when(t > 0)
-                def _():
-                    ring(t - 1, *turns[i - 2])
-
-    ring(jnp.int32(far), *turns[-2])
+                @pl.when(t == 0)
+                def _():
+                    ring(jnp.int32(0), u - 1, 0)
+
+                @pl.when(jnp.logical_and(t > 0, t < far))
+                def _():
+                    ring(t, u - 1, 1)
 
     def mates(h, u, way):
         ap_copy(h, u, way).wait_recv()
@@ -339,6 +351,7 @@
                 ag_copy(h - 1, u, way, False).wait_recv()
                 ag_copy(h, u, way, h == far - 1).start()
                 ap_copy(h, u, way).start()
+            for way in range(WAYS):
                 expand(slot_of(h, way), u, range(WAYS), ag, core)
                 if u == last:
                     expand_lone(slot_of(h, way), ag, core)
@@ -348,6 +361,7 @@
         for way in range(WAYS):
             ag_copy(far - 1, u, way, True).wait_recv()
             ap_copy(far, u, way, True).start()
+        for way in range(WAYS):
             expand(far, u, (way,), ag, core)
             mates(far - 1, u, way)
     expand_lone(far, ag, core)

time: 74.6 us -> 73.6 us (0.987)
  Pallas kernels: 71.8 us -> 70.8 us
    pallas_call x1, Pallas kernels: 71.8 us -> 70.8 us  [local_part(): pl.pallas_call(functools.partial(reduce_kernel, chips, n_seq, seq_len), o...]
where the time goes in v8:
time: 73.6 us; the launch traced here: 73.5 us
  Pallas kernels  70.8 us (96%)
  local copies, waits for them, and re-layouts  2.71 us (4%)
    pallas_call x1, Pallas kernels, local_part(): pl.pallas_call(functools.partial(reduce_kernel, chips, n_seq, seq_len), o...  70.8 us
    unnamed x1, local copies, waits for them, and re-layouts  2.71 us

profile of v8, /device:TPU:21, one launch (start us, length us, event | category | flops | bytes accessed | tf_op | source)
XLA Modules:
  0.0 73.5 jit_solution(10227607758572166640)
XLA Ops:
  0.0 70.8 %reduce_gather.1 = bf16[256,12288]{1,0:T(8,128)(2,1)S(1)} custom-call(s32[4]{0:T(128)} %len_ref.1, bf16[256,3072]{1,0:T(8,128)(2,1)} %x_hbm.1, bf16[3072,12288]{1,0:T(8,128)(2,1)} %w_hbm.1), custom_call_target="tpu_custom_call" | custom-call | tf_op jit(solution)/shard_map/reduce_gather/pallas_call | solution.py:419
  70.8 2.7 %copy.5 = bf16[256,12288]{1,0:T(8,128)(2,1)} copy(bf16[256,12288]{1,0:T(8,128)(2,1)S(1)} %reduce_gather.1) | data formatting | bytes 12582912

commit v9 on v8

--- a/solution.py
+++ b/solution.py
@@ -303,9 +303,6 @@
                 for way in range(WAYS):
                     ag_copy(0, u, way, False).start()
                 ap_copy(0, u, 0).start()
-                expand(0, u, range(WAYS), ag, core)
-                if u == last:
-                    expand_lone(0, ag, core)
 
     turns = [(u, side) for u in range(UNITS) for side in range(WAYS)]
 
@@ -345,6 +342,9 @@
         if u == last:
             expand_lone(slot_of(h, way), ag_pair, 1 - core)
 
+    for u in range(UNITS):
+        expand(0, u, range(WAYS), ag, core)
+    expand_lone(0, ag, core)
     for h in range(1, far):
         for u in range(UNITS):
             for way in range(WAYS):

time: 73.6 us -> 73.6 us (level)
  no operation moved by 1% of the time
where the time goes in v9:
time: 73.6 us; the launch traced here: 73.5 us
  Pallas kernels  70.8 us (96%)
  local copies, waits for them, and re-layouts  2.71 us (4%)
    pallas_call x1, Pallas kernels, local_part(): pl.pallas_call(functools.partial(reduce_kernel, chips, n_seq, seq_len), o...  70.8 us
    unnamed x1, local copies, waits for them, and re-layouts  2.71 us

profile of v9, /device:TPU:21, one launch (start us, length us, event | category | flops | bytes accessed | tf_op | source)
XLA Modules:
  0.0 73.5 jit_solution(3011556789210706074)
XLA Ops:
  0.0 70.8 %reduce_gather.1 = bf16[256,12288]{1,0:T(8,128)(2,1)S(1)} custom-call(s32[4]{0:T(128)} %len_ref.1, bf16[256,3072]{1,0:T(8,128)(2,1)} %x_hbm.1, bf16[3072,12288]{1,0:T(8,128)(2,1)} %w_hbm.1), custom_call_target="tpu_custom_call" | custom-call | tf_op jit(solution)/shard_map/reduce_gather/pallas_call | solution.py:419
  70.8 2.7 %copy.5 = bf16[256,12288]{1,0:T(8,128)(2,1)} copy(bf16[256,12288]{1,0:T(8,128)(2,1)S(1)} %reduce_gather.1) | data formatting | bytes 12582912
